TPU v7x, 32 devices: a whole 2x2x4 slice. The times are simulated.
32 devices in a mesh: seq: 4 (over z), shard: 8 (over y, x, core).
Axes of the slice: x: 2, y: 2, z: 4, core: 2. Of those that a mesh axis runs over, the one named last changes fastest.
Arguments:
- tokens: bfloat16 [2, 8, 2048, 768], P(None, 'shard', 'seq'), may hold values from -6 to 6
- lengths: int32 [8, 2], P('shard'), may hold values from 512 to 2048, as said below
- w_qkv: bfloat16 [768, 2304], P('shard'), may hold values from -0.21875 to 0.21875
- b_query: bfloat16 [768], P('shard'), may hold values from -3 to 3
- b_value: bfloat16 [768], P('shard'), may hold values from -3 to 3
- w_out: bfloat16 [768, 768], P('shard'), may hold values from -6 to 6
- b_out: bfloat16 [768], P('shard'), may hold values from -3 to 3
- gain_one: bfloat16 [768], P('shard'), may hold values from 0.5 to 1.5
- shift_one: bfloat16 [768], P('shard'), may hold values from -3 to 3
- w_up: bfloat16 [768, 3072], P('shard'), may hold values from -0.21875 to 0.21875
- b_up: bfloat16 [3072], P('shard'), may hold values from -3 to 3
- w_down: bfloat16 [3072, 768], P('shard'), may hold values from -0.109375 to 0.109375
- b_down: bfloat16 [768], P('shard'), may hold values from -3 to 3
- gain_two: bfloat16 [768], P('shard'), may hold values from 0.5 to 1.5
- shift_two: bfloat16 [768], P('shard'), may hold values from -3 to 3
- cotangent: bfloat16 [2, 8, 2048, 768], P(None, 'shard', 'seq'), may hold values from -6 to 6
Outputs:
- layer_out: bfloat16 [2, 8, 2048, 768], P(None, 'shard', 'seq')
- input_grad: bfloat16 [2, 8, 2048, 768], P(None, 'shard', 'seq')
- grad_w_qkv: float32 [768, 2304], P('shard')
- grad_b_query: float32 [768], P('shard')
- grad_b_value: float32 [768], P('shard')
- grad_w_out: float32 [768, 768], P('shard')
- grad_b_out: float32 [768], P('shard')
- grad_gain_one: float32 [768], P('shard')
- grad_shift_one: float32 [768], P('shard')
- grad_w_up: float32 [768, 3072], P('shard')
- grad_b_up: float32 [3072], P('shard')
- grad_w_down: float32 [3072, 768], P('shard')
- grad_b_down: float32 [768], P('shard')
- grad_gain_two: float32 [768], P('shard')
- grad_shift_two: float32 [768], P('shard')
Inputs may be any that keep to these rules, and one draw needn't show every extreme that they name: `lengths`: each group's sequence in each micro-batch has this many valid tokens at the start of its 2048 slots; some entry equals 2048.
All inputs are finite; a program needn't handle non-finite values.
Results may differ from a plain program's by a relative error of at most 0.015.
Values may be sent and summed in bfloat16 or wider, within the bound.
A program may use at most 192 MiB of HBM per device.

v0:
```python
import math

import jax
import jax.numpy as jnp
from jax import lax
from jax.sharding import PartitionSpec as P

H = 12


norm_eps = 1e-06


def layer_norm(inputs, scales, shifts):
    centre = jnp.mean(inputs, axis=-1, keepdims=True)
    centred = inputs - centre
    spread = jnp.mean(centred * centred, axis=-1, keepdims=True)
    return centred * lax.rsqrt(spread + norm_eps) * scales + shifts


def gelu_exact(inputs):
    return jax.nn.gelu(inputs, approximate=False)


def matmul_plain(left, right):
    return jnp.dot(left, right, preferred_element_type=jnp.float32)


def matmul_left_t(left, right):
    return lax.dot_general(
        left, right, (((0,), (0,)), ((), ())), preferred_element_type=jnp.float32
    )


def matmul_right_t(left, right):
    return lax.dot_general(
        left, right, (((1,), (1,)), ((), ())), preferred_element_type=jnp.float32
    )


def fetch_forward(
    w_qkv,
    b_query,
    b_value,
    w_out,
    b_out,
    gain_one,
    shift_one,
    w_up,
    b_up,
    w_down,
    b_down,
    gain_two,
    shift_two,
):
    return (
        lax.all_gather(w_qkv, "shard", axis=0, tiled=True),
        lax.all_gather(b_query, "shard", axis=0, tiled=True),
        lax.all_gather(b_value, "shard", axis=0, tiled=True),
        lax.all_gather(w_out, "shard", axis=0, tiled=True),
        lax.all_gather(b_out, "shard", axis=0, tiled=True),
        lax.all_gather(gain_one, "shard", axis=0, tiled=True),
        lax.all_gather(shift_one, "shard", axis=0, tiled=True),
        lax.all_gather(w_up, "shard", axis=0, tiled=True),
        lax.all_gather(b_up, "shard", axis=0, tiled=True),
        lax.all_gather(w_down, "shard", axis=0, tiled=True),
        lax.all_gather(b_down, "shard", axis=0, tiled=True),
        lax.all_gather(gain_two, "shard", axis=0, tiled=True),
        lax.all_gather(shift_two, "shard", axis=0, tiled=True),
    )


def fetch_backward(
    w_qkv,
    b_query,
    b_value,
    w_out,
    b_out,
    gain_one,
    shift_one,
    w_up,
    b_up,
    w_down,
    b_down,
    gain_two,
    shift_two,
):
    return (
        lax.all_gather(w_qkv, "shard", axis=0, tiled=True),
        lax.all_gather(b_query, "shard", axis=0, tiled=True),
        lax.all_gather(b_value, "shard", axis=0, tiled=True),
        lax.all_gather(w_out, "shard", axis=0, tiled=True),
        lax.all_gather(b_out, "shard", axis=0, tiled=True),
        lax.all_gather(gain_one, "shard", axis=0, tiled=True),
        lax.all_gather(shift_one, "shard", axis=0, tiled=True),
        lax.all_gather(w_up, "shard", axis=0, tiled=True),
        lax.all_gather(b_up, "shard", axis=0, tiled=True),
        lax.all_gather(w_down, "shard", axis=0, tiled=True),
        lax.all_gather(b_down, "shard", axis=0, tiled=True),
        lax.all_gather(gain_two, "shard", axis=0, tiled=True),
        lax.all_gather(shift_two, "shard", axis=0, tiled=True),
    )


def attention_forward(qkv_heads, seq_length):
    seq_slots, _, head_count, head_dim = qkv_heads.shape
    scaling = 1.0 / math.sqrt(head_dim)
    block_rows = min(512, seq_slots)
    queries = qkv_heads[:, 0].reshape(seq_slots // block_rows, block_rows, head_count, head_dim)
    key_rows = qkv_heads[:, 1]
    value_rows = qkv_heads[:, 2]
    key_valid = jnp.arange(seq_slots, dtype=jnp.int32) < seq_length

    def one_block(q_block):
        scores = (
            jnp.einsum("qhd,khd->hqk", q_block, key_rows, preferred_element_type=jnp.float32)
            * scaling
        )
        scores = jnp.where(key_valid[None, None, :], scores, -1e30)
        row_max = jnp.max(scores, axis=-1, keepdims=True)
        row_sum = jnp.sum(jnp.exp(scores - row_max), axis=-1, keepdims=True)
        log_total = row_max + jnp.log(row_sum)
        probs = jnp.exp(scores - log_total).astype(jnp.bfloat16)
        context = jnp.einsum("hqk,khd->qhd", probs, value_rows, preferred_element_type=jnp.float32)
        return (context.astype(jnp.bfloat16), log_total[..., 0])

    context, log_total = lax.map(one_block, queries)
    return (context.reshape(seq_slots, head_count * head_dim), log_total)


def attention_backward(qkv_heads, log_total, grad_context, seq_length):
    seq_slots, _, head_count, head_dim = qkv_heads.shape
    scaling = 1.0 / math.sqrt(head_dim)
    block_rows = min(512, seq_slots)
    block_count = seq_slots // block_rows
    queries = qkv_heads[:, 0].reshape(block_count, block_rows, head_count, head_dim)
    key_rows = qkv_heads[:, 1]
    value_rows = qkv_heads[:, 2]
    grad_blocks = grad_context.reshape(block_count, block_rows, head_count, head_dim)
    key_valid = jnp.arange(seq_slots, dtype=jnp.int32) < seq_length

    def one_block(carried, block_item):
        key_grad, value_grad = carried
        q_block, log_block, grad_block = block_item
        scores = (
            jnp.einsum("qhd,khd->hqk", q_block, key_rows, preferred_element_type=jnp.float32)
            * scaling
        )
        scores = jnp.where(key_valid[None, None, :], scores, -1e30)
        probs = jnp.exp(scores - log_block[..., None])
        grad_probs = jnp.einsum(
            "qhd,khd->hqk", grad_block, value_rows, preferred_element_type=jnp.float32
        )
        row_dot = jnp.sum(probs * grad_probs, axis=-1, keepdims=True)
        grad_scores = (probs * (grad_probs - row_dot)).astype(jnp.bfloat16)
        query_grad = (
            jnp.einsum("hqk,khd->qhd", grad_scores, key_rows, preferred_element_type=jnp.float32)
            * scaling
        )
        key_grad = (
            key_grad
            + jnp.einsum("hqk,qhd->khd", grad_scores, q_block, preferred_element_type=jnp.float32)
            * scaling
        )
        value_grad = value_grad + jnp.einsum(
            "hqk,qhd->khd",
            probs.astype(jnp.bfloat16),
            grad_block,
            preferred_element_type=jnp.float32,
        )
        return ((key_grad, value_grad), query_grad)

    zero_acc = jnp.zeros((seq_slots, head_count, head_dim), jnp.float32)
    (key_grad, value_grad), query_grad = lax.scan(
        one_block, (zero_acc, zero_acc), (queries, log_total, grad_blocks)
    )
    query_grad = query_grad.reshape(seq_slots, head_count, head_dim)
    return jnp.stack([query_grad, key_grad, value_grad], axis=1).astype(jnp.bfloat16)


def on_device(
    tokens,
    lengths,
    w_qkv,
    b_query,
    b_value,
    w_out,
    b_out,
    gain_one,
    shift_one,
    w_up,
    b_up,
    w_down,
    b_down,
    gain_two,
    shift_two,
    cotangent,
):
    micro_count = tokens.shape[0]
    tok_rows = tokens.shape[2]
    width = tokens.shape[3]
    seq_devices = lax.axis_size("seq")
    seq_place = lax.axis_index("seq")
    shard_count = lax.axis_size("shard")
    head_local = H // seq_devices
    head_dim = width // H
    seq_slots = tok_rows * seq_devices
    positions = seq_place * tok_rows + jnp.arange(tok_rows, dtype=jnp.int32)
    shards = (
        w_qkv,
        b_query,
        b_value,
        w_out,
        b_out,
        gain_one,
        shift_one,
        w_up,
        b_up,
        w_down,
        b_down,
        gain_two,
        shift_two,
    )
    grad_sums = [
        jnp.zeros((piece.shape[0] * shard_count,) + piece.shape[1:], jnp.float32)
        for piece in shards
    ]
    outputs = []
    input_grads = []
    for current in range(micro_count):
        weights_full = fetch_forward(*shards)
        (
            qkv_matrix,
            query_bias,
            value_bias,
            out_matrix,
            out_bias,
            gain_first,
            shift_first,
            up_matrix,
            up_bias,
            down_matrix,
            down_bias,
            gain_second,
            shift_second,
        ) = weights_full
        inputs_mb = tokens[current, 0]
        seq_length = lengths[0, current]
        row_valid = (positions < seq_length).astype(jnp.float32)[:, None]
        bias_all = jnp.concatenate([query_bias, jnp.zeros_like(query_bias), value_bias]).astype(
            jnp.float32
        )
        projected = (matmul_plain(inputs_mb, qkv_matrix) + bias_all).astype(jnp.bfloat16)
        qkv_heads = lax.all_to_all(
            projected.reshape(tok_rows, 3, seq_devices, head_local * head_dim),
            "seq",
            split_axis=2,
            concat_axis=0,
            tiled=True,
        )
        qkv_heads = qkv_heads.reshape(seq_slots, 3, head_local, head_dim)
        context_heads, log_total = attention_forward(qkv_heads, seq_length)
        context = lax.all_to_all(context_heads, "seq", split_axis=0, concat_axis=1, tiled=True)
        gain_first_f = gain_first.astype(jnp.float32)
        shift_first_f = shift_first.astype(jnp.float32)
        gain_second_f = gain_second.astype(jnp.float32)
        shift_second_f = shift_second.astype(jnp.float32)
        residual_one = (
            inputs_mb.astype(jnp.float32)
            + matmul_plain(context, out_matrix)
            + out_bias.astype(jnp.float32)
        )
        hidden_one = layer_norm(residual_one, gain_first_f, shift_first_f)
        hidden_low = hidden_one.astype(jnp.bfloat16)
        up_proj = matmul_plain(hidden_low, up_matrix) + up_bias.astype(jnp.float32)
        activated = gelu_exact(up_proj).astype(jnp.bfloat16)
        residual_two = (
            hidden_one + matmul_plain(activated, down_matrix) + down_bias.astype(jnp.float32)
        )
        outputs.append(layer_norm(residual_two, gain_second_f, shift_second_f).astype(jnp.bfloat16))
        weights_full = fetch_backward(*shards)
        (
            qkv_matrix,
            query_bias,
            value_bias,
            out_matrix,
            out_bias,
            gain_first,
            shift_first,
            up_matrix,
            up_bias,
            down_matrix,
            down_bias,
            gain_second,
            shift_second,
        ) = weights_full
        out_grad = cotangent[current, 0].astype(jnp.float32) * row_valid
        _, back_second = jax.vjp(layer_norm, residual_two, gain_second_f, shift_second_f)
        grad_residual_two, grad_gain_second, grad_shift_second = back_second(out_grad)
        down_grad = grad_residual_two.astype(jnp.bfloat16)
        grad_down = matmul_left_t(activated, down_grad)
        grad_down_bias = jnp.sum(down_grad.astype(jnp.float32), axis=0)
        _, back_gelu = jax.vjp(gelu_exact, up_proj)
        (grad_up_proj,) = back_gelu(matmul_right_t(down_grad, down_matrix))
        up_grad = grad_up_proj.astype(jnp.bfloat16)
        grad_up = matmul_left_t(hidden_low, up_grad)
        grad_up_bias = jnp.sum(up_grad.astype(jnp.float32), axis=0)
        grad_hidden_one = grad_residual_two + matmul_right_t(up_grad, up_matrix)
        _, back_first = jax.vjp(layer_norm, residual_one, gain_first_f, shift_first_f)
        grad_residual_one, grad_gain_first, grad_shift_first = back_first(grad_hidden_one)
        attn_grad = grad_residual_one.astype(jnp.bfloat16)
        grad_out = matmul_left_t(context, attn_grad)
        grad_out_bias = jnp.sum(attn_grad.astype(jnp.float32), axis=0)
        context_grad = matmul_right_t(attn_grad, out_matrix).astype(jnp.bfloat16)
        grad_heads = lax.all_to_all(context_grad, "seq", split_axis=1, concat_axis=0, tiled=True)
        grad_heads = grad_heads.reshape(seq_slots, head_local, head_dim)
        qkv_head_grad = attention_backward(qkv_heads, log_total, grad_heads, seq_length)
        qkv_grad = lax.all_to_all(
            qkv_head_grad.reshape(seq_slots, 3, 1, head_local * head_dim),
            "seq",
            split_axis=0,
            concat_axis=2,
            tiled=True,
        )
        qkv_grad = qkv_grad.reshape(tok_rows, 3 * width)
        grad_qkv = matmul_left_t(inputs_mb, qkv_grad)
        bias_grad_all = jnp.sum(qkv_grad.astype(jnp.float32), axis=0)
        input_grads.append(
            (grad_residual_one + matmul_right_t(qkv_grad, qkv_matrix)).astype(jnp.bfloat16)
        )
        terms = (
            grad_qkv,
            bias_grad_all[:width],
            bias_grad_all[2 * width :],
            grad_out,
            grad_out_bias,
            grad_gain_first,
            grad_shift_first,
            grad_up,
            grad_up_bias,
            grad_down,
            grad_down_bias,
            grad_gain_second,
            grad_shift_second,
        )
        grad_sums = [total + term for total, term in zip(grad_sums, terms)]
    shard_sums = (
        lax.psum_scatter(grad_sums[0], "shard", scatter_dimension=0, tiled=True),
        lax.psum_scatter(grad_sums[1], "shard", scatter_dimension=0, tiled=True),
        lax.psum_scatter(grad_sums[2], "shard", scatter_dimension=0, tiled=True),
        lax.psum_scatter(grad_sums[3], "shard", scatter_dimension=0, tiled=True),
        lax.psum_scatter(grad_sums[4], "shard", scatter_dimension=0, tiled=True),
        lax.psum_scatter(grad_sums[5], "shard", scatter_dimension=0, tiled=True),
        lax.psum_scatter(grad_sums[6], "shard", scatter_dimension=0, tiled=True),
        lax.psum_scatter(grad_sums[7], "shard", scatter_dimension=0, tiled=True),
        lax.psum_scatter(grad_sums[8], "shard", scatter_dimension=0, tiled=True),
        lax.psum_scatter(grad_sums[9], "shard", scatter_dimension=0, tiled=True),
        lax.psum_scatter(grad_sums[10], "shard", scatter_dimension=0, tiled=True),
        lax.psum_scatter(grad_sums[11], "shard", scatter_dimension=0, tiled=True),
        lax.psum_scatter(grad_sums[12], "shard", scatter_dimension=0, tiled=True),
    )
    summed = (
        lax.psum(shard_sums[0].astype(jnp.bfloat16), "seq").astype(jnp.float32),
        lax.psum(shard_sums[1].astype(jnp.bfloat16), "seq").astype(jnp.float32),
        lax.psum(shard_sums[2].astype(jnp.bfloat16), "seq").astype(jnp.float32),
        lax.psum(shard_sums[3].astype(jnp.bfloat16), "seq").astype(jnp.float32),
        lax.psum(shard_sums[4].astype(jnp.bfloat16), "seq").astype(jnp.float32),
        lax.psum(shard_sums[5].astype(jnp.bfloat16), "seq").astype(jnp.float32),
        lax.psum(shard_sums[6].astype(jnp.bfloat16), "seq").astype(jnp.float32),
        lax.psum(shard_sums[7].astype(jnp.bfloat16), "seq").astype(jnp.float32),
        lax.psum(shard_sums[8].astype(jnp.bfloat16), "seq").astype(jnp.float32),
        lax.psum(shard_sums[9].astype(jnp.bfloat16), "seq").astype(jnp.float32),
        lax.psum(shard_sums[10].astype(jnp.bfloat16), "seq").astype(jnp.float32),
        lax.psum(shard_sums[11].astype(jnp.bfloat16), "seq").astype(jnp.float32),
        lax.psum(shard_sums[12].astype(jnp.bfloat16), "seq").astype(jnp.float32),
    )
    layer_out = jnp.stack(outputs, axis=0)[:, None]
    input_grad = jnp.stack(input_grads, axis=0)[:, None]
    return (
        layer_out,
        input_grad,
        summed[0],
        summed[1],
        summed[2],
        summed[3],
        summed[4],
        summed[5],
        summed[6],
        summed[7],
        summed[8],
        summed[9],
        summed[10],
        summed[11],
        summed[12],
    )


def solution(mesh):
    placed = (
        P(None, "shard", "seq", None),
        P("shard", None),
        P("shard", None),
        P("shard"),
        P("shard"),
        P("shard", None),
        P("shard"),
        P("shard"),
        P("shard"),
        P("shard", None),
        P("shard"),
        P("shard", None),
        P("shard"),
        P("shard"),
        P("shard"),
        P(None, "shard", "seq", None),
    )
    return jax.shard_map(
        on_device,
        mesh=mesh,
        in_specs=placed,
        out_specs=(
            P(None, "shard", "seq", None),
            P(None, "shard", "seq", None),
            P("shard", None),
            P("shard"),
            P("shard"),
            P("shard", None),
            P("shard"),
            P("shard"),
            P("shard"),
            P("shard", None),
            P("shard"),
            P("shard", None),
            P("shard"),
            P("shard"),
            P("shard"),
        ),
        check_vma=False,
    )
```

profile of v0, /device:TPU:0, one launch (start us, length us, event | category | flops | bytes accessed | tf_op | source)
XLA Modules:
  0.0 961.6 jit_solution(3195086936663808667)
XLA Ops:
  16.6 27.1 %all-reduce.18 = (bf16[768]{0:T(1024)(128)(2,1)S(1)}, bf16[768]{0:T(1024)(128)(2,1)S(1)}, bf16[768]{0:T(1024)(128)(2,1)}, bf16[768]{0:T(1024)(128)(2,1)}, bf16[7...) all-reduce(bf16[768]{0:T(1024)(128)(2,1)S(1)} %dynamic-update-slice, ...), channel_id=1, replica_groups=mesh['seq'=4,'shard'=8] {'shard'}, use_global_device_ids=true, to_apply=%add.1 | all-reduce | flops 6144 | bytes 24576
  76.9 39.0 %all-to-all-done = bf16[512,3,4,192]{0,3,1,2:T(8,128)(2,1)S(1)} async-done(((bf16[512,3,4,192]{0,3,1,2:T(8,128)(2,1)}), bf16[512,3,4,192]{0,3,1,2:T(8,128)(2,1)S(1)}, u32[]{:S(2)}, u32[]{:S(2)}) %all-to-all-start) | async-done | bytes 2359328 | tf_op jit(solution)/shard_map/all_to_all | solution.py:254
  133.3 36.4 %while.56 = (s32[]{:T(128)}, bf16[4,512,3,64]{1,3,2,0:T(8,128)(2,1)}, f32[4,3,512]{2,1,0:T(4,128)S(1)}, bf16[4,512,3,64]{1,3,2,0:T(8,128)(2,1)S(1)}, bf16[2048,3...) while((s32[]{:T(128)}, ...), condition=%wide.region_3.4_spmd.clone, body=%wide.region_0.3_spmd.clone.sunk | while | flops 840008192 | bytes 39780960 | solution.py:127
  192.3 34.0 %while.57 = (s32[]{:T(128)}, bf16[4,512,3,64]{1,3,2,0:T(8,128)(2,1)S(1)}, f32[4,3,512]{2,1,0:T(4,128)S(1)}, bf16[4,512,3,64]{1,3,2,0:T(8,128)(2,1)S(1)}, bf16[20...) while((s32[]{:T(128)}, ...), condition=%wide.region_11.12_spmd.clone, body=%wide.region_8.11_spmd.clone.sunk | while | flops 840008192 | bytes 39782500 | solution.py:127
  232.9 8.8 all-gather
  262.9 34.8 %multiply_convert_fusion.3 = (bf16[512,3072]{1,0:T(8,128)(2,1)}, f32[512,3072]{1,0:T(8,128)}, bf16[512,3072]{1,0:T(8,128)(2,1)}, f32[512,3072]{1,0:T(8,128)}, f32[512,3072]{1,0:T(8,128)}) fusion(f32[3072]{0:T(1024)S(1)} %bitcast.336, f32[512,3072]{1,0:T(8,128)S(1)} %fusion.144, bf16[768,3072]{1,0:T(8,128)(2,1)S(1)} %copy-done.66, ...), kind=kOutput, calls=%fused_computation.126 | convolution fusion | flops 2625503232 | bytes 37771264 | tf_op jit(solution)/shard_map/dot_general | solution.py:26
  320.2 18.1 %convert_reduce_fusion.1 = (f32[3072]{0:T(1024)}, bf16[512,3072]{1,0:T(8,128)(2,1)}, f32[3072]{0:T(1024)}, bf16[512,3072]{1,0:T(8,128)(2,1)}) fusion(f32[512,3072]{1,0:T(8,128)} %get-tuple-element.761, f32[512,3072]{1,0:T(8,128)} %get-tuple-element.802, f32[3072]{0:T(1024)S(1)} %bitcast.337, f32[512,3072]{1,0:T(8,128)} %fusion.162, ...), kind=kOutput, calls=%fused_computation.110 | convolution fusion | flops 2469390336 | bytes 43290624 | tf_op jit(solution)/shard_map/dot_general | solution.py:36
  344.4 6.4 multiply_reduce_fusion.3
  380.0 9.0 fusion.146
  393.0 8.9 convolution_add_fusion.1
  408.2 124.5 %while.58 = (s32[]{:T(128)}, f32[2048,3,64]{0,2,1:T(8,128)S(1)}, f32[2048,3,64]{0,2,1:T(8,128)}, bf16[4,512,3,64]{1,3,2,0:T(8,128)(2,1)}, bf16[4,512,3,64]{1,3,2...) while((s32[]{:T(128)}, f32[2048,3,64]{0,2,1:T(8,128)S(1)}, ...), condition=%wide.region_22.23_spmd.clone, body=%wide.region_20.22_spmd.clone.sunk | while | flops 2062516736 | bytes 204919504 | solution.py:174
  427.4 7.0 fusion.273
  458.0 6.4 fusion.273
  488.6 7.4 fusion.273
  520.7 6.4 fusion.273
  548.5 120.6 %while.59 = (s32[]{:T(128)}, f32[2048,3,64]{0,2,1:T(8,128)S(1)}, f32[2048,3,64]{0,2,1:T(8,128)}, bf16[4,512,3,64]{1,3,2,0:T(8,128)(2,1)}, bf16[4,512,3,64]{1,3,2...) while((s32[]{:T(128)}, f32[2048,3,64]{0,2,1:T(8,128)S(1)}, ...), condition=%wide.region_29.30_spmd.clone, body=%wide.region_27.29_spmd.clone.sunk | while | flops 2062516736 | bytes 204919504 | solution.py:174
  683.3 7.8 copy.160
  691.1 81.0 %all-to-all-done.7 = bf16[2048,3,1,192]{3,1,2,0:T(4,128)(2,1)} async-done(((bf16[2048,3,1,192]{3,1,2,0:T(4,128)(2,1)}), bf16[2048,3,1,192]{3,1,2,0:T(4,128)(2,1)}, u32[]{:S(2)}, u32[]{:S(2)}) %all-to-all-start.7) | async-done | bytes 2359328 | tf_op jit(solution)/shard_map/all_to_all | solution.py:318
  772.1 7.2 copy.161
  791.1 8.0 copy.162
  812.9 50.6 %reduce-scatter.13.cloned.1.call-done = f32[96,2304]{1,0:T(8,128)} async-done(((f32[768,2304]{1,0:T(8,128)}), f32[96,2304]{1,0:T(8,128)}) %reduce-scatter.13.cloned.1.call-update) | async-done | bytes 884752
  867.2 24.6 %all-reduce.17 = (bf16[768]{0:T(1024)(128)(2,1)S(1)}, bf16[768]{0:T(1024)(128)(2,1)S(1)}, bf16[768]{0:T(1024)(128)(2,1)S(1)}, bf16[768]{0:T(1024)(128)(2,1)S(1)}...) all-reduce(f32[768]{0:T(1024)S(1)} %add.360, ...), channel_id=3, replica_groups=mesh['seq'=4,'shard'=8] {'shard'}, use_global_device_ids=true, to_apply=%region_34.35.clone | all-reduce | flops 9216 | bytes 55296
  892.5 12.8 %all-reduce.19 = (bf16[96]{0:T(256)(128)(2,1)S(1)}, bf16[96]{0:T(256)(128)(2,1)S(1)}, bf16[96]{0:T(256)(128)(2,1)S(1)}, bf16[96]{0:T(256)(128)(2,1)S(1)}, bf16[9...) all-reduce(bf16[96]{0:T(256)(128)(2,1)S(1)} %dynamic-slice.43, ...), channel_id=1, replica_groups=mesh['seq'=4,'shard'=8] {'seq'}, use_global_device_ids=true, to_apply=%region_35.36 | all-reduce | flops 1152 | bytes 4608 | tf_op jit(solution)/shard_map/psum | solution.py:364
  919.1 29.5 %all-reduce.23.cloned.1.call-done = (bf16[96,2304]{0,1:T(8,128)(2,1)}, bf16[96,768]{1,0:T(8,128)(2,1)}, bf16[96,3072]{1,0:T(8,128)(2,1)}, bf16[384,768]{1,0:T(8,128)(2,1)}) async-done(((bf16[96,2304]{0,1:T(8,128)(2,1)}, bf16[96,768]{1,0:T(8,128)(2,1)}, bf16[96,3072]{1,0:T(8,128)(2,1)}, bf16[384,768]{1,0:T(8,128)(2,1)}), (bf16[96,2304]{0,1:T(8,128)(2,1)}, bf16[96,768]{1,0:T(8,128)(2,1)}, ...) | async-done | bytes 1769488 | tf_op jit(solution)/shard_map/psum | solution.py:363
  (465 shorter events, 542.6 us)
Async XLA Ops:
  7.2 39.5 %all-gather.6.cloned.1.call-start = ((), (), s32[]{:S(2)}) async-start(), calls=%async_computation.12 | async-start | bytes 3981312 | tf_op jit(solution)/shard_map/all_gather | solution.py:57
  56.9 59.0 %all-to-all-start = ((bf16[512,3,4,192]{0,3,1,2:T(8,128)(2,1)}), bf16[512,3,4,192]{0,3,1,2:T(8,128)(2,1)S(1)}, u32[]{:S(2)}, u32[]{:S(2)}) async-start(bf16[512,3,4,192]{0,3,1,2:T(8,128)(2,1)} %copy.136), calls=%async_computation | async-start | bytes 4718592 | tf_op jit(solution)/shard_map/all_to_all | solution.py:254
  61.7 181.5 %all-gather.8.cloned.1.call-start = ((), (), s32[]{:S(2)}) async-start(), calls=%async_computation.13 | async-start | bytes 1327104 | tf_op jit(solution)/shard_map/all_gather | solution.py:60
  62.4 192.8 %all-gather.10.cloned.1.call-start = ((), (), s32[]{:S(2)}) async-start(), calls=%async_computation.14 | async-start | bytes 5308416 | tf_op jit(solution)/shard_map/all_gather | solution.py:64
  115.9 58.2 %all-to-all-start.2 = ((bf16[512,3,4,192]{0,3,1,2:T(8,128)(2,1)}), bf16[512,3,4,192]{0,3,1,2:T(8,128)(2,1)}, u32[]{:S(2)}, u32[]{:S(2)}) async-start(bf16[512,3,4,192]{0,3,1,2:T(8,128)(2,1)} %copy.140), calls=%async_computation.2 | async-start | bytes 4718592 | tf_op jit(solution)/shard_map/all_to_all | solution.py:254
  174.1 52.2 %all-to-all-start.1 = ((bf16[4,512,192]{1,2,0:T(8,128)(2,1)}), bf16[4,512,192]{1,2,0:T(8,128)(2,1)}, u32[]{:S(2)}, u32[]{:S(2)}) async-start(bf16[4,512,192]{1,2,0:T(8,128)(2,1)} %bitcast.8), calls=%async_computation.1 | async-start | bytes 1572864 | tf_op jit(solution)/shard_map/all_to_all | solution.py:263
  192.2 40.6 %copy-start.62 = (bf16[768]{0:T(1024)(128)(2,1)S(1)}, bf16[768]{0:T(1024)(128)(2,1)}, u32[]{:S(2)}) copy-start(bf16[768]{0:T(1024)(128)(2,1)} %get-tuple-element.719) | copy-start | bytes 4612
  192.3 40.6 %copy-start.61 = (bf16[768]{0:T(1024)(128)(2,1)S(1)}, bf16[768]{0:T(1024)(128)(2,1)}, u32[]{:S(2)}) copy-start(bf16[768]{0:T(1024)(128)(2,1)} %get-tuple-element.718) | copy-start | bytes 4612
  192.3 40.6 %copy-start.65 = (bf16[384]{0:T(512)(128)(2,1)S(1)}, bf16[384]{0:T(512)(128)(2,1)}, u32[]{:S(2)}) copy-start(bf16[384]{0:T(512)(128)(2,1)} %param.34) | copy-start | bytes 2308
  192.3 49.5 %copy-start.60 = (bf16[768]{0:T(1024)(128)(2,1)S(1)}, bf16[768]{0:T(1024)(128)(2,1)}, u32[]{:S(2)}) copy-start(bf16[768]{0:T(1024)(128)(2,1)} %get-tuple-element.720) | copy-start | bytes 4612
  192.3 49.5 %copy-start.59 = (bf16[768]{0:T(1024)(128)(2,1)S(1)}, bf16[768]{0:T(1024)(128)(2,1)}, u32[]{:S(2)}) copy-start(bf16[768]{0:T(1024)(128)(2,1)} %get-tuple-element.721) | copy-start | bytes 4612
  192.3 49.5 %copy-start.58 = (bf16[768]{0:T(1024)(128)(2,1)S(1)}, bf16[768]{0:T(1024)(128)(2,1)}, u32[]{:S(2)}) copy-start(bf16[768]{0:T(1024)(128)(2,1)} %get-tuple-element.722) | copy-start | bytes 4612
  227.2 24.2 %all-to-all-start.3 = ((bf16[4,512,192]{1,2,0:T(8,128)(2,1)}), bf16[4,512,192]{1,2,0:T(8,128)(2,1)S(1)}, u32[]{:S(2)}, u32[]{:S(2)}) async-start(bf16[4,512,192]{1,2,0:T(8,128)(2,1)} %bitcast.331), calls=%async_computation.3 | async-start | bytes 1572864 | tf_op jit(solution)/shard_map/all_to_all | solution.py:263
  232.2 65.4 %all-gather.12.cloned.1.call-start = ((), (), s32[]{:S(2)}) async-start(), calls=%async_computation.15 | async-start | bytes 5308416 | tf_op jit(solution)/shard_map/all_gather | solution.py:66
  232.8 570.6 %reduce-scatter.7.cloned.1.call-start = ((), (), s32[]{:S(2)}) async-start(), calls=%async_computation.16 | async-start | bytes 2654208 | tf_op jit(solution)/shard_map/reduce_scatter | solution.py:351
  359.9 448.4 %reduce-scatter.11.cloned.1.call-start = ((), (), s32[]{:S(2)}) async-start(), calls=%async_computation.18 | async-start | bytes 10616832 | tf_op jit(solution)/shard_map/reduce_scatter | solution.py:357
  375.7 26.2 %all-to-all-start.4 = ((bf16[512,4,192]{0,2,1:T(8,128)(2,1)}), bf16[512,4,192]{0,2,1:T(8,128)(2,1)}, u32[]{:S(2)}, u32[]{:S(2)}) async-start(bf16[512,4,192]{0,2,1:T(8,128)(2,1)} %bitcast.330), calls=%async_computation.4 | async-start | bytes 1572864 | tf_op jit(solution)/shard_map/all_to_all | solution.py:315
  379.9 430.7 %reduce-scatter.9.cloned.1.call-start = ((), (), s32[]{:S(2)}) async-start(), calls=%async_computation.17 | async-start | bytes 10616832 | tf_op jit(solution)/shard_map/reduce_scatter | solution.py:355
  401.9 139.8 %all-to-all-start.6 = ((bf16[512,4,192]{0,2,1:T(8,128)(2,1)}), bf16[512,4,192]{0,2,1:T(8,128)(2,1)}, u32[]{:S(2)}, u32[]{:S(2)}) async-start(bf16[512,4,192]{0,2,1:T(8,128)(2,1)} %bitcast.329), calls=%async_computation.6 | async-start | bytes 1572864 | tf_op jit(solution)/shard_map/all_to_all | solution.py:315
  541.7 136.4 %all-to-all-start.5 = ((bf16[2048,3,1,192]{3,1,2,0:T(4,128)(2,1)}), bf16[2048,3,1,192]{3,1,2,0:T(4,128)(2,1)}, u32[]{:S(2)}, u32[]{:S(2)}) async-start(bf16[2048,3,1,192]{3,1,2,0:T(4,128)(2,1)} %copy.146), calls=%async_computation.5 | async-start | bytes 8388608 | tf_op jit(solution)/shard_map/all_to_all | solution.py:318
  678.1 94.0 %all-to-all-start.7 = ((bf16[2048,3,1,192]{3,1,2,0:T(4,128)(2,1)}), bf16[2048,3,1,192]{3,1,2,0:T(4,128)(2,1)}, u32[]{:S(2)}, u32[]{:S(2)}) async-start(bf16[2048,3,1,192]{3,1,2,0:T(4,128)(2,1)} %copy.152), calls=%async_computation.7 | async-start | bytes 8388608 | tf_op jit(solution)/shard_map/all_to_all | solution.py:318
  683.3 180.2 %reduce-scatter.13.cloned.1.call-start = ((), (), s32[]{:S(2)}) async-start(), calls=%async_computation.19 | async-start | bytes 7962624
  799.3 149.2 %all-reduce.23.cloned.1.call-start = ((), (), s32[]{:S(2)}) async-start(), calls=%async_computation.20 | async-start | bytes 3833856 | tf_op jit(solution)/shard_map/psum | solution.py:363
  812.9 97.1 %copy-start.53 = (f32[512]{0:T(512)S(1)}, f32[512]{0:T(512)}, u32[]{:S(2)}) copy-start(f32[512]{0:T(512)} %copy-done.52) | copy-start | bytes 6148
  (78 other events, 525.1 us)
Sparse Core Ops, SparseCore 0:
  9.9 36.7 all-gather.5
  64.4 24.3 all-gather.7
  90.7 38.7 all-gather.9
  234.6 39.2 all-gather.11
  360.0 40.3 reduce-scatter.6
  403.8 76.8 reduce-scatter.10
  484.1 76.8 reduce-scatter.8
  799.4 64.0 reduce-scatter.12
  867.3 81.2 all-reduce.22
where the time goes:
time: 971 us; the launch traced here: 962 us
  matrix products  389 us (40%)
  waiting for transfers between devices  215 us (22%)
  other arithmetic  115 us (12%)
  local copies, waits for them, and re-layouts  112 us (12%)
  blocking collectives  73.4 us (8%)
  starting transfers between devices  40 us (4%)
  between operations  17.3 us (2%)
    all_to_all x2, waiting for transfers between devices, on_device(): lax.all_to_all(qkv_head_grad.reshape(seq_slots, 3, 1, head_local * head_d...  81 us
    dot_general x8, matrix products, matmul_plain(): return jnp.dot(left, right, preferred_element_type=jnp.float32)  66.5 us
    unnamed x10, waiting for transfers between devices  53.3 us
    dot_general x8, matrix products, one_block(): jnp.einsum('hqk,khd->qhd', grad_scores, key_rows, preferred_element_type=...  52.3 us
    unnamed x2, blocking collectives  51.8 us
    dot_general x8, matrix products, matmul_right_t(): lax.dot_general(left, right, (((1,), (1,)), ((), ())), preferred_element_...  47.5 us
    all_to_all x2, waiting for transfers between devices, on_device(): lax.all_to_all(projected.reshape(tok_rows, 3, seq_devices, head_local * h...  43.5 us
    dot_general x8, matrix products, one_block(): jnp.einsum('hqk,qhd->khd', probs.astype(jnp.bfloat16), grad_block, prefer...  43.4 us
  transfers between devices with their start and end apart: 17, of which 7 were waited for; matrix products, arithmetic and copies ran while one was open for 55% of the time, Pallas kernels for 0%

commit v1 on v0

v1 whole, which is shorter than its diff:
```python
import functools
import math

import jax
import jax.numpy as jnp
from jax import lax
from jax.sharding import PartitionSpec as P
from jax.experimental import pallas as pl
from jax.experimental.pallas import tpu as pltpu

LANES = 128
f32 = jnp.float32
bf16 = jnp.bfloat16


def dot_nt(a, b):
    return lax.dot_general(a, b, (((1,), (1,)), ((), ())), preferred_element_type=f32)


def dot_tn(a, b):
    return lax.dot_general(a, b, (((0,), (0,)), ((), ())), preferred_element_type=f32)


def dot_nn(a, b):
    return jnp.dot(a, b, preferred_element_type=f32)


def keys_of_head(keys, length, head):
    shape = keys.shape
    lane = lax.broadcasted_iota(jnp.int32, shape, 1)
    row = lax.broadcasted_iota(jnp.int32, shape, 0)
    half = LANES // 2
    spare = half * (1 - head)
    bias = jnp.where(row < length, 0.0, -1e30).astype(f32)
    kept = jnp.where((lane // half) == head, keys.astype(f32), 0.0)
    return jnp.where(lane == spare, bias, kept).astype(bf16)


def rows_of_head(rows, head, spare_value):
    lane = lax.broadcasted_iota(jnp.int32, rows.shape, 1)
    half = LANES // 2
    kept = jnp.where((lane // half) == head, rows.astype(f32), 0.0)
    if spare_value:
        kept = jnp.where(lane == half * (1 - head), spare_value, kept)
    return kept.astype(bf16)


def attn_fwd_kernel(len_ref, order_ref, q_ref, k_ref, v_ref, o_ref, lse_ref, key_scr, val_scr, s_scr, *, chunk):
    slots = k_ref.shape[0]
    rows = q_ref.shape[0]

    @pl.when(pl.program_id(1) == 0)
    def _():
        for head in range(2):
            key_scr[head] = keys_of_head(k_ref[...], len_ref[0], head)
        val_scr[:, :LANES] = v_ref[...]
        val_scr[:, LANES:] = jnp.ones((slots, LANES), bf16)

    queries = q_ref[...]
    lane = lax.broadcasted_iota(jnp.int32, (rows, LANES), 1)
    result = None
    for head in range(2):
        qa = rows_of_head(queries, head, 1.0)
        top = None
        for start in range(0, slots, chunk):
            s = dot_nt(qa, key_scr[head, start : start + chunk, :])
            s_scr[head, :, start : start + chunk] = s
            for part in range(0, chunk, LANES):
                piece = s[:, part : part + LANES]
                top = piece if top is None else jnp.maximum(top, piece)
        top = jnp.max(top, axis=1, keepdims=True)
        acc = None
        for start in range(0, slots, chunk):
            p = jnp.exp(s_scr[head, :, start : start + chunk] - top).astype(bf16)
            term = dot_nn(p, val_scr[start : start + chunk, :])
            acc = term if acc is None else acc + term
        total = acc[:, LANES:]
        out = acc[:, :LANES] / total
        lse = jnp.transpose(jnp.broadcast_to(top, (rows, LANES)) + jnp.log(total))
        lse_ref[0, head : head + 1, :] = lse[0:1, :]
        result = out if result is None else jnp.where(lane < LANES // 2, result, out)
    o_ref[...] = result.astype(bf16)


def attention_forward(qkv, length, order, rows, chunk=512):
    slots, width = qkv.shape
    pairs = width // (3 * LANES)
    blocks = order.shape[0]
    return pl.pallas_call(
        functools.partial(attn_fwd_kernel, chunk=chunk),
        out_shape=(
            jax.ShapeDtypeStruct((blocks * rows, pairs * LANES), bf16),
            jax.ShapeDtypeStruct((pairs, 8, blocks * rows), f32),
        ),
        grid_spec=pltpu.PrefetchScalarGridSpec(
            num_scalar_prefetch=2,
            grid=(pairs, blocks),
            in_specs=[
                pl.BlockSpec((rows, LANES), lambda g, i, n, o: (o[i], g)),
                pl.BlockSpec((slots, LANES), lambda g, i, n, o: (0, pairs + g)),
                pl.BlockSpec((slots, LANES), lambda g, i, n, o: (0, 2 * pairs + g)),
            ],
            out_specs=[
                pl.BlockSpec((rows, LANES), lambda g, i, n, o: (i, g)),
                pl.BlockSpec((1, 8, rows), lambda g, i, n, o: (g, 0, i)),
            ],
            scratch_shapes=[
                pltpu.VMEM((2, slots, LANES), bf16),
                pltpu.VMEM((slots, 2 * LANES), bf16),
                pltpu.VMEM((2, rows, slots), f32),
            ],
        ),
        compiler_params=pltpu.CompilerParams(
            dimension_semantics=("arbitrary", "arbitrary"), vmem_limit_bytes=48 << 20
        ),
        cost_estimate=pl.CostEstimate(
            flops=16 * blocks * rows * slots * pairs * LANES,
            transcendentals=2 * pairs * slots * blocks * rows,
            bytes_accessed=2 * slots * width * 2,
        ),
        name="attn_fwd",
    )(length, order, qkv, qkv, qkv)


def attn_bwd_kernel(
    len_ref, order_ref, q_ref, k_ref, v_ref, o_ref, do_ref, lse_ref,
    dq_ref, dk_ref, dv_ref, key_scr, dk_scr, dv_scr, *, chunk, scaling,
):
    slots = k_ref.shape[0]
    step = pl.program_id(1)

    @pl.when(step == 0)
    def _():
        for head in range(2):
            key_scr[head] = keys_of_head(k_ref[...], len_ref[0], head)
        dk_scr[...] = jnp.zeros_like(dk_scr)
        dv_scr[...] = jnp.zeros_like(dv_scr)

    queries = q_ref[...]
    grads = do_ref[...]
    prod = grads.astype(f32) * o_ref[...].astype(f32)
    lane8 = lax.broadcasted_iota(jnp.int32, (8, LANES), 1)
    dq = None
    for head in range(2):
        pick = jnp.where((lane8 // (LANES // 2)) == head, 1.0, 0.0).astype(f32)
        delta = lax.dot_general(
            pick, prod, (((1,), (1,)), ((), ())),
            precision=lax.Precision.HIGHEST, preferred_element_type=f32,
        )[0:1, :]
        lse = lse_ref[0, head : head + 1, :]
        qx = rows_of_head(queries, head, 1.0)
        qa = rows_of_head(queries, head, 0.0)
        da = rows_of_head(grads, head, 0.0)
        for start in range(0, slots, chunk):
            here = slice(start, start + chunk)
            keys = key_scr[head, here, :]
            p = jnp.exp(dot_nt(keys, qx) - lse)
            ds = (p * (dot_nt(v_ref[here, :], da) - delta)).astype(bf16)
            dv_scr[here, :] += dot_nn(p.astype(bf16), da)
            dk_scr[here, :] += dot_nn(ds, qa)
            term = dot_tn(ds, keys)
            dq = term if dq is None else dq + term
    dq_ref[...] = (dq * scaling).astype(bf16)

    @pl.when(step == pl.num_programs(1) - 1)
    def _():
        dk_ref[...] = dk_scr[...].astype(bf16)
        dv_ref[...] = dv_scr[...].astype(bf16)


def attention_backward(qkv, length, order, context, grad, lse, scaling, rows, chunk=1024):
    slots, width = qkv.shape
    pairs = width // (3 * LANES)
    shape = jax.ShapeDtypeStruct((slots, pairs * LANES), bf16)
    return pl.pallas_call(
        functools.partial(attn_bwd_kernel, chunk=chunk, scaling=scaling),
        out_shape=(shape, shape, shape),
        grid_spec=pltpu.PrefetchScalarGridSpec(
            num_scalar_prefetch=2,
            grid=(pairs, slots // rows),
            in_specs=[
                pl.BlockSpec((rows, LANES), lambda g, i, n, o: (o[i], g)),
                pl.BlockSpec((slots, LANES), lambda g, i, n, o: (0, pairs + g)),
                pl.BlockSpec((slots, LANES), lambda g, i, n, o: (0, 2 * pairs + g)),
                pl.BlockSpec((rows, LANES), lambda g, i, n, o: (i, g)),
                pl.BlockSpec((rows, LANES), lambda g, i, n, o: (i, g)),
                pl.BlockSpec((1, 8, rows), lambda g, i, n, o: (g, 0, i)),
            ],
            out_specs=[
                pl.BlockSpec((rows, LANES), lambda g, i, n, o: (o[i], g)),
                pl.BlockSpec((slots, LANES), lambda g, i, n, o: (0, g)),
                pl.BlockSpec((slots, LANES), lambda g, i, n, o: (0, g)),
            ],
            scratch_shapes=[
                pltpu.VMEM((2, slots, LANES), bf16),
                pltpu.VMEM((slots, LANES), f32),
                pltpu.VMEM((slots, LANES), f32),
            ],
        ),
        compiler_params=pltpu.CompilerParams(
            dimension_semantics=("arbitrary", "arbitrary"), vmem_limit_bytes=48 << 20
        ),
        cost_estimate=pl.CostEstimate(
            flops=40 * slots * slots * pairs * LANES,
            transcendentals=2 * pairs * slots * slots,
            bytes_accessed=4 * slots * width * 2,
        ),
        name="attn_bwd",
    )(length, order, qkv, qkv, qkv, context, grad, lse)


H = 12
norm_eps = 1e-06
ERF_P = 0.32
ERF_C = (
    0.18140208045914907,
    0.16781523017336925,
    0.2520604501706694,
    -0.13396961774602328,
    0.7456596101028902,
    -0.724323250347485,
    0.6843514662938643,
    -0.17299593051459605,
)


def gelu_parts(u):
    t = 1.0 / (1.0 + (ERF_P / math.sqrt(2.0)) * jnp.abs(u))
    bell = jnp.exp(-0.5 * u * u)
    poly = ERF_C[-1]
    for coefficient in ERF_C[-2::-1]:
        poly = poly * t + coefficient
    tail = 0.5 * poly * t * bell
    phi = jnp.where(u >= 0, 1.0 - tail, tail)
    return u * phi, phi + u * bell * (1.0 / math.sqrt(2.0 * math.pi))


def norm_parts(rows):
    centred = rows - jnp.mean(rows, axis=-1, keepdims=True)
    scale = lax.rsqrt(jnp.mean(centred * centred, axis=-1, keepdims=True) + norm_eps)
    return centred * scale, scale


def norm_back(grad, normed, scale, gain):
    e = grad * gain
    return scale * (
        e
        - jnp.mean(e, axis=-1, keepdims=True)
        - normed * jnp.mean(e * normed, axis=-1, keepdims=True)
    )


class Lines:
    def __init__(self):
        self.n_seq = lax.axis_size("seq")
        self.n_shard = lax.axis_size("shard")
        self.z = lax.axis_index("seq")
        self.shard = lax.axis_index("shard")
        self.core = lax.rem(self.shard, 2)

    def device(self, z, shard):
        return z * self.n_shard + shard

    def towards(self, step):
        pairs = []
        for z in range(self.n_seq):
            for shard in range(self.n_shard):
                p = (z + step) % self.n_seq
                there = self.device(2 * (p // 2) + shard % 2, 2 * (shard // 2) + p % 2)
                pairs.append((self.device(z, shard), there))
        return pairs

    def send(self, piece, step):
        return lax.ppermute(piece, ("seq", "shard"), self.towards(step))

    def send_back(self, piece, step):
        return lax.ppermute(piece, ("seq", "shard"), [(b, a) for a, b in self.towards(step)])

    def swap(self, piece):
        return lax.ppermute(piece, "shard", [(k, k ^ 1) for k in range(self.n_shard)])

    def target(self, step):
        return lax.rem(self.z + step, self.n_seq)

    def source(self, step, core):
        return lax.rem(2 * (self.z // 2) + core - step + self.n_seq, self.n_seq)


def put(whole, piece, *starts):
    return lax.dynamic_update_slice(whole, piece, starts)


def layer(
    tokens,
    lengths,
    w_qkv,
    b_query,
    b_value,
    w_out,
    b_out,
    gain_one,
    shift_one,
    w_up,
    b_up,
    w_down,
    b_down,
    gain_two,
    shift_two,
    cotangent,
):
    lines = Lines()
    micro, _, rows, width = tokens.shape
    n_seq, n_shard, core = lines.n_seq, lines.n_shard, lines.core
    assert micro * 2 == n_seq
    half_rows = rows // 2
    half = width // 2
    hidden = w_up.shape[1]
    slots = rows * n_seq
    scaling = 1.0 / math.sqrt(width // H)
    parity = [[k for k in range(n_shard) if k % 2 == c] for c in range(2)]

    x_home = tokens[:, 0].reshape(n_seq, half_rows, width)
    x_seq = jnp.zeros((slots, width), bf16)
    for step in range(n_seq):
        piece = lines.send(
            lax.dynamic_index_in_dim(x_home, lines.target(step), 0, keepdims=False), step
        )
        other = lines.swap(piece)
        own_at = lines.source(step, core) * rows + core * half_rows
        other_at = lines.source(step, 1 - core) * rows + (1 - core) * half_rows
        x_seq = put(x_seq, piece, own_at, 0)
        x_seq = put(x_seq, other, other_at, 0)
    there = lines.swap(lengths)
    length = jnp.where(lax.rem(lines.z, 2) == core, lengths, there)
    length = lax.dynamic_index_in_dim(length[0], lines.z // 2, 0)

    small = jnp.concatenate(
        [b_query, b_value, b_out, gain_one, shift_one, b_down, gain_two, shift_two, b_up]
    )
    small_rows = -(-small.shape[0] // (3 * half))
    small = jnp.pad(small, (0, small_rows * 3 * half - small.shape[0]))
    shard_rows = w_qkv.shape[0]
    extra = -(-small_rows // 16) * 16
    columns = w_qkv.reshape(shard_rows, 3, 2, half)
    small = jnp.pad(small.reshape(small_rows, 3 * half), ((0, extra - small_rows), (0, 0)))

    def package(which):
        picked = lax.dynamic_index_in_dim(columns, which, 2, keepdims=False)
        return jnp.concatenate([picked.reshape(shard_rows, 3 * half), small])

    mine, theirs = package(core), lines.swap(package(1 - core))
    both = jnp.stack(
        [jnp.where(core == 0, mine, theirs), jnp.where(core == 0, theirs, mine)]
    )
    everyone = lax.all_gather(both, "shard", axis_index_groups=parity, axis=0, tiled=True)
    qkv_matrix = everyone[:, :shard_rows].reshape(width, 3 * half)
    vectors = everyone[:, shard_rows : shard_rows + small_rows].reshape(n_shard, -1)
    vectors = vectors.astype(f32)
    per = width // n_shard

    def vector(place):
        return vectors[:, place * per : (place + 1) * per].reshape(width)

    query_bias, value_bias, out_bias, gain_first, shift_first, down_bias, gain_second, shift_second = (
        vector(place) for place in range(8)
    )
    up_bias = vectors[:, 8 * per : 8 * per + hidden // n_shard].reshape(hidden)

    out_matrix = lax.all_gather(w_out, "shard", axis=0, tiled=True)
    up_matrix = lax.all_gather(w_up, "shard", axis=0, tiled=True)
    down_matrix = lax.all_gather(w_down, "shard", axis=0, tiled=True)

    head_bias = jnp.concatenate(
        [
            lax.dynamic_slice(query_bias, (core * half,), (half,)),
            jnp.zeros((half,), f32),
            lax.dynamic_slice(value_bias, (core * half,), (half,)),
        ]
    )
    head_scale = jnp.where(jnp.arange(3 * half) < half, scaling, 1.0).astype(f32)
    qkv = (
        (dot_nn(x_seq, qkv_matrix) + head_bias).astype(bf16).astype(f32) * head_scale
    ).astype(bf16)
    order = jnp.stack([lines.source(step, core) for step in range(n_seq)]).astype(jnp.int32)
    blocks, parts, log_totals = [], [], []
    for first in range(0, n_seq, 2):
        block, log_total = attention_forward(qkv, length, order[first : first + 2], rows)
        log_totals.append(log_total)
        blocks.append(block)
        for step in (first, first + 1):
            parts.append(lines.send_back(block[(step - first) * rows :][:rows], step))
    context_seq = jnp.concatenate(blocks)
    log_total = jnp.concatenate(log_totals, axis=2)
    parts = jnp.stack(parts + parts)
    parts = lax.dynamic_slice_in_dim(parts, lax.rem(n_seq - lines.z, n_seq), n_seq)
    parts = parts.reshape(micro, 2, rows, half)
    left, right = (parts[:, k].reshape(micro * rows, half) for k in range(2))

    inputs = tokens[:, 0].reshape(micro * rows, width).astype(f32)
    positions = lines.z * rows + jnp.arange(rows, dtype=jnp.int32)
    row_valid = (positions[None, :] < lengths[0][:, None]).reshape(micro * rows, 1)
    residual_one = inputs + dot_nn(left, out_matrix[:half]) + dot_nn(right, out_matrix[half:]) + out_bias
    normed_one, scale_one = norm_parts(residual_one)
    hidden_one = normed_one * gain_first + shift_first
    hidden_low = hidden_one.astype(bf16)
    up_proj = dot_nn(hidden_low, up_matrix) + up_bias
    activated, slope = gelu_parts(up_proj)
    activated, slope = lax.optimization_barrier((activated.astype(bf16), slope))
    residual_two = hidden_one + dot_nn(activated, down_matrix) + down_bias
    normed_two, scale_two = norm_parts(residual_two)
    layer_out = (normed_two * gain_second + shift_second).astype(bf16)

    out_grad = jnp.where(
        row_valid, cotangent[:, 0].reshape(micro * rows, width).astype(f32), 0.0
    )
    grad_two = norm_back(out_grad, normed_two, scale_two, gain_second)
    down_grad = grad_two.astype(bf16)
    up_grad = (dot_nt(down_grad, down_matrix) * slope).astype(bf16)
    grad_hidden = grad_two + dot_nt(up_grad, up_matrix)
    grad_one = norm_back(grad_hidden, normed_one, scale_one, gain_first)
    attn_grad = grad_one.astype(bf16)
    context_grad = dot_nt(attn_grad, out_matrix).astype(bf16)

    arrived = []
    for step in range(n_seq):
        target = lines.target(step)
        block = lax.dynamic_slice(
            context_grad, ((target // 2) * rows, lax.rem(target, 2) * half), (rows, half)
        )
        arrived.append(lines.send(block, step))
    context_grad_seq = jnp.concatenate(arrived)

    def by_shard(matrix):
        return matrix.reshape((n_shard, -1) + matrix.shape[1:])

    def column_sum(values):
        return jnp.sum(values.astype(f32), axis=0)

    small_grads = [
        column_sum(attn_grad),
        column_sum(grad_hidden * normed_one),
        column_sum(grad_hidden),
        column_sum(down_grad),
        column_sum(out_grad * normed_two),
        column_sum(out_grad),
        column_sum(up_grad),
    ]
    small_grads = jnp.concatenate([by_shard(g) for g in small_grads], axis=1)
    tail_rows = -(-small_grads.shape[1] // width)
    tail_rows = -(-tail_rows // 16) * 16
    small_grads = jnp.pad(
        small_grads, ((0, 0), (0, tail_rows * width - small_grads.shape[1]))
    ).reshape(n_shard, tail_rows, width)
    grad_up = by_shard(dot_tn(hidden_low, up_grad))
    grad_down = by_shard(dot_tn(activated, down_grad))
    grad_out = dot_tn(left, attn_grad)
    grad_out = by_shard(jnp.concatenate([grad_out, dot_tn(right, attn_grad)]))
    bundle = jnp.concatenate(
        [grad_up[..., k * width :][..., :width] for k in range(hidden // width)]
        + [grad_down, grad_out, small_grads],
        axis=1,
    ).astype(bf16)

    def reduce_shard(pieces, groups=None):
        flat = pieces.reshape((-1,) + pieces.shape[2:])
        return lax.psum_scatter(
            flat, "shard", scatter_dimension=0, axis_index_groups=groups, tiled=True
        )

    context_grad_seq, bundle = lax.optimization_barrier((context_grad_seq, bundle))
    bundle = reduce_shard(bundle)

    grad_query, grad_key, grad_value = attention_backward(
        qkv, length, order, context_seq, context_grad_seq, log_total, scaling, rows
    )
    qkv_grad = jnp.concatenate([grad_query, grad_key, grad_value], axis=1)
    by_half = qkv_grad.reshape(n_seq, 2, half_rows, 3 * half)

    def half_of_rows(which):
        picked = lax.dynamic_index_in_dim(by_half, which, 1, keepdims=False)
        return dot_nt(picked.reshape(-1, 3 * half), qkv_matrix)

    given = half_of_rows(1 - core).astype(bf16)
    given = lines.swap(given)
    joined = (half_of_rows(core) + given.astype(f32)).astype(bf16)
    joined = joined.reshape(n_seq, half_rows, width)
    back = jnp.zeros((n_seq, half_rows, width), bf16)
    for step in range(n_seq):
        block = lax.dynamic_index_in_dim(joined, lines.source(step, core), 0)
        block = lines.send_back(block, step)
        back = put(back, block, lines.target(step), 0, 0)
    input_grad = (grad_one + back.reshape(micro * rows, width).astype(f32)).astype(bf16)

    pair_rows = 2 * shard_rows
    groups = n_shard // 2
    bias_rows = jnp.pad(
        jnp.broadcast_to(column_sum(qkv_grad), (groups, 1, 3 * half)), ((0, 0), (0, 15), (0, 0))
    )
    grad_qkv = dot_tn(x_seq, qkv_grad).reshape(groups, pair_rows, 3 * half)
    grad_qkv = jnp.concatenate([grad_qkv, bias_rows], axis=1).astype(bf16)
    grad_qkv = reduce_shard(grad_qkv, parity)
    grad_qkv, bundle = lax.psum((grad_qkv, bundle), "seq")
    bundle = bundle.astype(f32)
    bias_row = grad_qkv[pair_rows : pair_rows + 16]
    own = lax.dynamic_slice(grad_qkv, (core * shard_rows, 0), (shard_rows, 3 * half))
    other = lax.dynamic_slice(grad_qkv, ((1 - core) * shard_rows, 0), (shard_rows, 3 * half))
    mine = jnp.concatenate([own, bias_row])
    theirs = lines.swap(jnp.concatenate([other, bias_row]))
    halves = jnp.stack(
        [jnp.where(core == 0, mine, theirs), jnp.where(core == 0, theirs, mine)], axis=1
    ).astype(f32)
    halves = halves.reshape(-1, 2, 3, half).transpose(0, 2, 1, 3).reshape(-1, 3 * width)
    grad_w_qkv = halves[:shard_rows]
    bias_grad = halves[shard_rows]
    mine_at = lines.shard * per
    grad_b_query = lax.dynamic_slice(bias_grad, (mine_at,), (per,))
    grad_b_value = lax.dynamic_slice(bias_grad, (2 * width + mine_at,), (per,))

    edges = [shard_rows * k for k in range(hidden // width + 1)]
    grad_up = jnp.concatenate(
        [bundle[a:b] for a, b in zip(edges, edges[1:])], axis=1
    )
    down_at = edges[-1]
    out_at = down_at + hidden // n_shard
    tail_at = out_at + shard_rows
    tail = bundle[tail_at:].reshape(-1)
    grad_b_out, grad_gain_one, grad_shift_one, grad_b_down, grad_gain_two, grad_shift_two = (
        tail[place * per : (place + 1) * per] for place in range(6)
    )
    grad_b_up = tail[6 * per : 6 * per + hidden // n_shard]
    return (
        layer_out.reshape(tokens.shape),
        input_grad.reshape(tokens.shape),
        grad_w_qkv,
        grad_b_query,
        grad_b_value,
        bundle[out_at:tail_at],
        grad_b_out,
        grad_gain_one,
        grad_shift_one,
        grad_up,
        grad_b_up,
        bundle[down_at:out_at],
        grad_b_down,
        grad_gain_two,
        grad_shift_two,
    )


def solution(mesh):
    placed = (
        P(None, "shard", "seq", None),
        P("shard", None),
        P("shard", None),
        P("shard"),
        P("shard"),
        P("shard", None),
        P("shard"),
        P("shard"),
        P("shard"),
        P("shard", None),
        P("shard"),
        P("shard", None),
        P("shard"),
        P("shard"),
        P("shard"),
        P(None, "shard", "seq", None),
    )
    return jax.shard_map(
        layer,
        mesh=mesh,
        in_specs=placed,
        out_specs=(
            P(None, "shard", "seq", None),
            P(None, "shard", "seq", None),
            P("shard", None),
            P("shard"),
            P("shard"),
            P("shard", None),
            P("shard"),
            P("shard"),
            P("shard"),
            P("shard", None),
            P("shard"),
            P("shard", None),
            P("shard"),
            P("shard"),
            P("shard"),
        ),
        check_vma=False,
    )
```

time: 971 us -> 651 us (0.67)
  matrix products: 389 us -> 94.2 us
  Pallas kernels: 0 us -> 132 us
  other arithmetic: 115 us -> 23.1 us
  blocking collectives: 73.4 us -> 0 us
  waiting for transfers between devices: 215 us -> 274 us
  local copies, waits for them, and re-layouts: 112 us -> 62.5 us
    dot_general x80 -> x15, matrix products: 389 us -> 94.2 us  [the longest x5 42.7 us: dot_nn(): return jnp.dot(a, b, preferred_element_type=f32)]
    pallas_call x0 -> x3, Pallas kernels: none -> 132 us  [the longest x1 80 us: attention_backward(): pl.pallas_call(functools.partial(attn_bwd_kernel, chunk=chunk, scaling=sc...]
    all_to_all x8 -> x0, waiting for transfers between devices: 129 us -> none  [the longest x2 81 us: on_device(): lax.all_to_all(qkv_head_grad.reshape(seq_slots, 3, 1, head_local * head_d...]
    ppermute x0 -> x24, waiting for transfers between devices: none -> 127 us  [the longest x8 82.7 us: send_back(): lax.ppermute(piece, ('seq', 'shard'), [(b, a) for a, b in self.towards(st...]
    reduce_scatter x3 -> x1, waiting for transfers between devices: 0.02 us -> 87 us  [reduce_shard(): lax.psum_scatter(flat, 'shard', scatter_dimension=0, axis_index_groups=gr...]
    convert_element_type x32 -> x2, other arithmetic: 57.2 us -> 2.78 us  [the longest x1 1.68 us: layer(): (grad_one + back.reshape(micro * rows, width).astype(f32)).astype(bf16)]
    unnamed x2 -> x0, blocking collectives: 51.8 us -> none
    ppermute x0 -> x24, starting transfers between devices: none -> 42.6 us  [the longest x8 19 us: swap(): lax.ppermute(piece, 'shard', [(k, k ^ 1) for k in range(self.n_shard)])]
  transfers between devices with their start and end apart: 17 -> 31, of which waited for: 7 -> 11; matrix products, arithmetic and copies ran while one was open for 55% -> 13% of each run, Pallas kernels for 0% -> 8%
where the time goes in v1:
time: 651 us; the launch traced here: 644 us
  waiting for transfers between devices  274 us (42%)
  Pallas kernels  132 us (20%)
  matrix products  94.2 us (14%)
  local copies, waits for them, and re-layouts  62.5 us (10%)
  starting transfers between devices  42.9 us (7%)
  other arithmetic  23.1 us (4%)
  between operations  15.7 us (2%)
    reduce_scatter x1, waiting for transfers between devices, reduce_shard(): lax.psum_scatter(flat, 'shard', scatter_dimension=0, axis_index_groups=gr...  87 us
    ppermute x8, waiting for transfers between devices, send_back(): lax.ppermute(piece, ('seq', 'shard'), [(b, a) for a, b in self.towards(st...  82.7 us
    pallas_call x1, Pallas kernels, attention_backward(): pl.pallas_call(functools.partial(attn_bwd_kernel, chunk=chunk, scaling=sc...  80 us
    pallas_call x2, Pallas kernels, attention_forward(): pl.pallas_call(functools.partial(attn_fwd_kernel, chunk=chunk), out_shape...  51.5 us
    dot_general x5, matrix products, dot_nn(): return jnp.dot(a, b, preferred_element_type=f32)  42.7 us
    ppermute x8, waiting for transfers between devices, send(): return lax.ppermute(piece, ('seq', 'shard'), self.towards(step))  42.7 us
    psum x1, waiting for transfers between devices, layer(): grad_qkv, bundle = lax.psum((grad_qkv, bundle), 'seq')  32.8 us
    dot_general x5, matrix products, dot_nt(): lax.dot_general(a, b, (((1,), (1,)), ((), ())), preferred_element_type=f32)  30 us
  transfers between devices with their start and end apart: 31, of which 11 were waited for; matrix products, arithmetic and copies ran while one was open for 13% of the time, Pallas kernels for 8%

profile of v1, /device:TPU:0, one launch (start us, length us, event | category | flops | bytes accessed | tf_op | source)
XLA Modules:
  0.0 644.4 jit_solution(16337255665235501174)
XLA Ops:
  11.3 6.1 concatenate.52
  33.8 13.2 %collective-permute-done.3 = bf16[256,768]{1,0:T(8,128)(2,1)} collective-permute-done((bf16[256,768]{1,0:T(8,128)(2,1)S(1)}, bf16[256,768]{1,0:T(8,128)(2,1)}, u32[]{:S(2)}, u32[]{:S(2)}) %collective-permute-start.3) | collective-permute-done | bytes 393248 | tf_op jit(solution)/shard_map/ppermute | solution.py:274
  47.6 8.3 %collective-permute-done.5 = bf16[256,768]{1,0:T(8,128)(2,1)} collective-permute-done((bf16[256,768]{1,0:T(8,128)(2,1)S(1)}, bf16[256,768]{1,0:T(8,128)(2,1)}, u32[]{:S(2)}, u32[]{:S(2)}) %collective-permute-start.5) | collective-permute-done | bytes 393248 | tf_op jit(solution)/shard_map/ppermute | solution.py:274
  55.9 7.7 %collective-permute-start.8 = (bf16[256,768]{1,0:T(8,128)(2,1)S(1)}, bf16[256,768]{1,0:T(8,128)(2,1)S(1)}, u32[]{:S(2)}, u32[]{:S(2)}) collective-permute-start(bf16[256,768]{1,0:T(8,128)(2,1)S(1)} %collective-permute-done.7), channel_id=1, source_target_pairs={{0,1},{1,0},{2,3},{3,2},{4,5},{5,4},{6,7},{7,6},{8,9},{9,8},{10,11... | collective-permute-start | bytes 1179656 | tf_op jit(solution)/shard_map/ppermute | solution.py:280
  72.5 5.5 multiply_convert_fusion.2.q_ref.k_ref.v_ref
  78.0 25.8 %attn_fwd.2 = (bf16[1024,384]{1,0:T(8,128)(2,1)S(1)}, f32[3,8,1024]{2,1,0:T(8,128)S(1)}) custom-call(s32[1]{0:T(128)} %bitcast.1.len_ref, s32[2]{0:T(128)S(1)} %get-tuple-element.171.order_ref, bf16[2048,1152]{1,0:T(8,128)(2,1)S(1)} %multiply_convert_fusion.2.q_ref.k_ref.v_ref, bf16[2048,1152]{1,0:T(8,128)(2,1)S(1)} %multiply_convert_fusion.2.q_ref.k_ref.v_ref, ...), custom_call_target="tpu_custom_call" | custom-call | flops 12884901888 | bytes 9437184 | tf_op jit(solution)/shard_map/attn_fwd/pallas_call | solution.py:89
  104.8 25.8 %attn_fwd.3 = (bf16[1024,384]{1,0:T(8,128)(2,1)S(1)}, f32[3,8,1024]{2,1,0:T(8,128)S(1)}) custom-call(s32[1]{0:T(128)} %bitcast.1.len_ref, s32[2]{0:T(128)S(1)} %get-tuple-element.172.order_ref, bf16[2048,1152]{1,0:T(8,128)(2,1)S(1)} %multiply_convert_fusion.2.q_ref.k_ref.v_ref, bf16[2048,1152]{1,0:T(8,128)(2,1)S(1)} %multiply_convert_fusion.2.q_ref.k_ref.v_ref, ...), custom_call_target="tpu_custom_call" | custom-call | flops 12884901888 | bytes 9437184 | tf_op jit(solution)/shard_map/attn_fwd/pallas_call | solution.py:89
  148.7 24.5 %collective-permute-done.12 = bf16[512,384]{1,0:T(8,128)(2,1)S(1)} collective-permute-done((bf16[512,384]{1,0:T(8,128)(2,1)}, bf16[512,384]{1,0:T(8,128)(2,1)S(1)}, u32[]{:S(2)}, u32[]{:S(2)}) %collective-permute-start.12) | collective-permute-done | bytes 393248 | tf_op jit(solution)/shard_map/ppermute | solution.py:277
  180.6 23.3 %fusion.4 = (f32[1024,3072]{1,0:T(8,128)}, bf16[1024,3072]{1,0:T(8,128)(2,1)}) fusion(f32[3072]{0:T(1024)S(1)} %copy-done.21, bf16[768,3072]{1,0:T(8,128)(2,1)} %all-gather.9.cloned.1.call-done, f32[1024,768]{1,0:T(8,128)S(1)} %get-tuple-element.165, f32[768]{0:T(1024)S(1)} %copy-done.24, f32[768]{0:T(1024)S(1)} %mul.284, f32[1024]{0:T(1024)S(1)} %add_rsqrt_fusion.1, ...), kind=kOutput, calls=%fused_computation.6 | convolution fusion | flops 4936433664 | bytes 26765312 | tf_op jit(solution)/shard_map/dot_general | solution.py:25
  203.9 8.9 %fusion.35 = (f32[1024]{0:T(1024)S(1)}, f32[1024,768]{1,0:T(8,128)S(1)}) fusion(f32[768]{0:T(1024)S(1)} %copy-done.25, bf16[1024,3072]{1,0:T(8,128)(2,1)} %get-tuple-element.28, bf16[3072,768]{1,0:T(8,128)(2,1)} %all-gather.11.cloned.1.call-done, f32[768]{0:T(1024)S(1)} %copy-done.24, f32[768]{0:T(1024)S(1)} %mul.284, f32[1024]{0:T(1024)S(1)} %add_rsqrt_fusion.1, ...), kind=kOutput, calls=%fused_computation.147 | convolution fusion | flops 4837342208 | bytes 17323008 | tf_op jit(solution)/shard_map/dot_general | solution.py:25
  218.2 11.2 %fusion.36 = (bf16[3072]{0:T(1024)(128)(2,1)S(1)}, bf16[1024,3072]{1,0:T(8,128)(2,1)}) fusion(f32[1024,3072]{1,0:T(8,128)} %get-tuple-element.29, bf16[3072,768]{1,0:T(8,128)(2,1)} %all-gather.11.cloned.1.call-done, f32[1024,768]{1,0:T(8,128)S(1)} %get-tuple-element.110), kind=kOutput, calls=%fused_computation.148 | convolution fusion | flops 4842058752 | bytes 26744832 | tf_op jit(solution)/shard_map/dot_general | solution.py:17
  229.4 9.8 %multiply_reduce_fusion.1 = (bf16[768]{0:T(1024)(128)(2,1)S(1)}, f32[1024]{0:T(1024)S(1)}, f32[1024]{0:T(1024)S(1)}, bf16[768]{0:T(1024)(128)(2,1)S(1)}, f32[1024,768]{1,0:T(8,128)S(1)}) fusion(f32[1024,768]{1,0:T(8,128)S(1)} %get-tuple-element.165, f32[1024]{0:T(1024)S(1)} %add_rsqrt_fusion.1, f32[1024]{0:T(1024)S(1)} %broadcast_multiply_fusion.4, ...), kind=kOutput, calls=%fused_computation.24 | convolution fusion | flops 4839698432 | bytes 20469760 | tf_op jit(solution)/shard_map/dot_general | solution.py:17
  243.5 9.0 %convolution_convert_fusion = bf16[3072,768]{1,0:T(8,128)(2,1)S(1)} fusion(bf16[1024,3072]{1,0:T(8,128)(2,1)} %get-tuple-element.28, f32[1024,768]{1,0:T(8,128)S(1)} %get-tuple-element.110), kind=kOutput, calls=%fused_computation.11 | convolution fusion | flops 4834983936 | bytes 14155776 | tf_op jit(solution)/shard_map/dot_general | solution.py:21
  252.6 6.5 %convolution_convert_fusion.1 = bf16[768,3072]{1,0:T(8,128)(2,1)S(1)} fusion(bf16[1024,3072]{1,0:T(8,128)(2,1)S(1)} %bitcast.147, f32[1024,768]{1,0:T(8,128)S(1)} %get-tuple-element.165, f32[768]{0:T(1024)S(1)} %copy-done.24, f32[768]{0:T(1024)S(1)} %mul.284, f32[1024]{0:T(1024)S(1)} %add_rsqrt_fusion.1, f32[1024]{0:T(1024)S(1)} %broadcast_multiply_fusion.4), kind=kOutput, calls=%fused_computation.12 | convolution fusion | flops 4838129664 | bytes 14170112 | tf_op jit(solution)/shard_map/dot_general | solution.py:21
  272.9 12.5 %collective-permute-done.15 = bf16[512,384]{1,0:T(8,128)(2,1)} collective-permute-done((bf16[512,384]{1,0:T(8,128)(2,1)S(1)}, bf16[512,384]{1,0:T(8,128)(2,1)}, u32[]{:S(2)}, u32[]{:S(2)}) %collective-permute-start.15) | collective-permute-done | bytes 393248 | tf_op jit(solution)/shard_map/ppermute | solution.py:274
  285.4 8.7 %collective-permute-done.16 = bf16[512,384]{1,0:T(8,128)(2,1)} collective-permute-done((bf16[512,384]{1,0:T(8,128)(2,1)S(1)}, bf16[512,384]{1,0:T(8,128)(2,1)}, u32[]{:S(2)}, u32[]{:S(2)}) %collective-permute-start.16) | collective-permute-done | bytes 393248 | tf_op jit(solution)/shard_map/ppermute | solution.py:274
  296.6 80.0 %attn_bwd.1 = (bf16[2048,384]{1,0:T(8,128)(2,1)S(1)}, bf16[2048,384]{1,0:T(8,128)(2,1)S(1)}, bf16[2048,384]{1,0:T(8,128)(2,1)S(1)}) custom-call(s32[1]{0:T(128)} %bitcast.1.len_ref, s32[4]{0:T(128)S(1)} %pad_add_fusion.2.order_ref, bf16[2048,1152]{1,0:T(8,128)(2,1)} %copy-done, bf16[2048,1152]{1,0:T(8,128)(2,1)} %copy-done, bf16[2048,1152]{1,0:T(8,128)(2,1)} %copy-done, ...), custom_call_target="tpu_custom_call" | custom-call | flops 64424509440 | bytes 18874368 | tf_op jit(solution)/shard_map/attn_bwd/pallas_call | solution.py:175
  395.5 8.0 %collective-permute-start.18 = (bf16[1024,768]{1,0:T(8,128)(2,1)}, bf16[1024,768]{1,0:T(8,128)(2,1)}, u32[]{:S(2)}, u32[]{:S(2)}) collective-permute-start(bf16[1024,768]{1,0:T(8,128)(2,1)} %convolution_convert_fusion.3), channel_id=1, source_target_pairs={{0,1},{1,0},{2,3},{3,2},{4,5},{5,4},{6,7},{7,6},{8,9},{9,8},{10,11... | collective-permute-start | bytes 4718600 | tf_op jit(solution)/shard_map/ppermute | solution.py:280
  403.5 26.2 %reduce-scatter.7.cloned.1.call-done = bf16[208,1152]{1,0:T(8,128)(2,1)} async-done(((bf16[832,1152]{1,0:T(8,128)(2,1)}), bf16[208,1152]{1,0:T(8,128)(2,1)}) %reduce-scatter.7.cloned.1.call-update) | async-done | bytes 479248
  429.7 87.0 %reduce-scatter.5.cloned.1.call-done = bf16[880,768]{1,0:T(8,128)(2,1)} async-done(((bf16[7040,768]{1,0:T(8,128)(2,1)}), bf16[880,768]{1,0:T(8,128)(2,1)}) %reduce-scatter.5.cloned.1.call-update) | async-done | bytes 1351696 | tf_op jit(solution)/shard_map/reduce_scatter | solution.py:466
  522.1 4.8 collective-permute-start.19
  531.2 14.7 %collective-permute-done.20 = bf16[1,256,768]{2,1,0:T(8,128)(2,1)} collective-permute-done((bf16[1,256,768]{2,1,0:T(8,128)(2,1)}, bf16[1,256,768]{2,1,0:T(8,128)(2,1)}, u32[]{:S(2)}, u32[]{:S(2)}) %collective-permute-start.20) | collective-permute-done | bytes 393248 | tf_op jit(solution)/shard_map/ppermute | solution.py:277
  546.9 43.5 %collective-permute-done.21 = bf16[1,256,768]{2,1,0:T(8,128)(2,1)} collective-permute-done((bf16[1,256,768]{2,1,0:T(8,128)(2,1)}, bf16[1,256,768]{2,1,0:T(8,128)(2,1)}, u32[]{:S(2)}, u32[]{:S(2)}) %collective-permute-start.21) | collective-permute-done | bytes 393248 | tf_op jit(solution)/shard_map/ppermute | solution.py:277
  593.2 32.8 %all-reduce.7.cloned.1.call-done = (bf16[880,768]{1,0:T(8,128)(2,1)}, bf16[208,1152]{1,0:T(8,128)(2,1)}) async-done(((bf16[880,768]{1,0:T(8,128)(2,1)}, bf16[208,1152]{1,0:T(8,128)(2,1)}), (bf16[880,768]{1,0:T(8,128)(2,1)}, bf16[208,1152]{1,0:T(8,128)(2,1)})) %all-reduce.7.cloned.1.call-update) | async-done | bytes 1830928 | tf_op jit(solution)/shard_map/psum | solution.py:502
  (249 shorter events, 125.0 us)
Async XLA Ops:
  7.2 61.0 %all-gather.5.cloned.1.call-start = ((), (), s32[]{:S(2)}) async-start(), calls=%async_computation.2 | async-start | bytes 2580480 | tf_op jit(solution)/shard_map/all_gather | solution.py:355
  20.1 154.7 %all-gather.7.cloned.1.call-start = ((), (), s32[]{:S(2)}) async-start(), calls=%async_computation.3 | async-start | bytes 1327104 | tf_op jit(solution)/shard_map/all_gather | solution.py:369
  20.8 159.6 %all-gather.9.cloned.1.call-start = ((), (), s32[]{:S(2)}) async-start(), calls=%async_computation.4 | async-start | bytes 5308416 | tf_op jit(solution)/shard_map/all_gather | solution.py:370
  21.6 182.3 %all-gather.11.cloned.1.call-start = ((), (), s32[]{:S(2)}) async-start(), calls=%async_computation.5 | async-start | bytes 5308416 | tf_op jit(solution)/shard_map/all_gather | solution.py:371
  23.2 23.8 %collective-permute-start.3 = (bf16[256,768]{1,0:T(8,128)(2,1)S(1)}, bf16[256,768]{1,0:T(8,128)(2,1)}, u32[]{:S(2)}, u32[]{:S(2)}) collective-permute-start(bf16[256,768]{1,0:T(8,128)(2,1)S(1)} %get-tuple-element.131), channel_id=1, source_target_pairs={{0,1},{1,9},{2,3},{3,11},{4,5},{5,13},{6,7},{7,15},{8,16},{9,24},{... | collective-permute-start | bytes 1179656 | tf_op jit(solution)/shard_map/ppermute | solution.py:274
  26.8 29.1 %collective-permute-start.5 = (bf16[256,768]{1,0:T(8,128)(2,1)S(1)}, bf16[256,768]{1,0:T(8,128)(2,1)}, u32[]{:S(2)}, u32[]{:S(2)}) collective-permute-start(bf16[256,768]{1,0:T(8,128)(2,1)S(1)} %get-tuple-element.130), channel_id=1, source_target_pairs={{0,16},{1,24},{2,18},{3,26},{4,20},{5,28},{6,22},{7,30},{8,17},{9,... | collective-permute-start | bytes 1179656 | tf_op jit(solution)/shard_map/ppermute | solution.py:274
  29.4 26.5 %collective-permute-start.7 = (bf16[256,768]{1,0:T(8,128)(2,1)S(1)}, bf16[256,768]{1,0:T(8,128)(2,1)S(1)}, u32[]{:S(2)}, u32[]{:S(2)}) collective-permute-start(bf16[256,768]{1,0:T(8,128)(2,1)S(1)} %get-tuple-element.129), channel_id=1, source_target_pairs={{0,17},{1,25},{2,19},{3,27},{4,21},{5,29},{6,23},{7,31},{8,0},{9,8... | collective-permute-start | bytes 1179656 | tf_op jit(solution)/shard_map/ppermute | solution.py:274
  29.4 17.6 %collective-permute-start = (s32[1,2]{1,0:T(1,128)S(1)}, s32[1,2]{1,0:T(1,128)S(1)}, u32[]{:S(2)}, u32[]{:S(2)}) collective-permute-start(s32[1,2]{1,0:T(1,128)S(1)} %copy-done.26), channel_id=1, source_target_pairs={{0,1},{1,0},{2,3},{3,2},{4,5},{5,4},{6,7},{7,6},{8,9},{9,8},{10,11... | collective-permute-start | bytes 32 | tf_op jit(solution)/shard_map/ppermute | solution.py:280
  31.4 398.3 %reduce-scatter.7.cloned.1.call-start = ((), (), s32[]{:S(2)}) async-start(), calls=%async_computation.7 | async-start | bytes 2396160
  32.2 32.6 %collective-permute-start.2 = (bf16[256,768]{1,0:T(8,128)(2,1)}, bf16[256,768]{1,0:T(8,128)(2,1)}, u32[]{:S(2)}, u32[]{:S(2)}) collective-permute-start(bf16[256,768]{1,0:T(8,128)(2,1)} %collective-permute-done.1), channel_id=1, source_target_pairs={{0,1},{1,0},{2,3},{3,2},{4,5},{5,4},{6,7},{7,6},{8,9},{9,8},{10,11... | collective-permute-start | bytes 1179656 | tf_op jit(solution)/shard_map/ppermute | solution.py:280
  47.0 19.9 %collective-permute-start.4 = (bf16[256,768]{1,0:T(8,128)(2,1)}, bf16[256,768]{1,0:T(8,128)(2,1)S(1)}, u32[]{:S(2)}, u32[]{:S(2)}) collective-permute-start(bf16[256,768]{1,0:T(8,128)(2,1)} %collective-permute-done.3), channel_id=1, source_target_pairs={{0,1},{1,0},{2,3},{3,2},{4,5},{5,4},{6,7},{7,6},{8,9},{9,8},{10,11... | collective-permute-start | bytes 1179656 | tf_op jit(solution)/shard_map/ppermute | solution.py:280
  132.8 15.7 %collective-permute-start.10 = (bf16[512,384]{1,0:T(8,128)(2,1)}, bf16[512,384]{1,0:T(8,128)(2,1)S(1)}, u32[]{:S(2)}, u32[]{:S(2)}) collective-permute-start(bf16[512,384]{1,0:T(8,128)(2,1)} %get-tuple-element.141), channel_id=1, source_target_pairs={{0,0},{8,1},{2,2},{10,3},{4,4},{12,5},{6,6},{14,7},{1,8},{9,9},{3,... | collective-permute-start | bytes 1179656 | tf_op jit(solution)/shard_map/ppermute | solution.py:277
  134.5 14.1 %collective-permute-start.11 = (bf16[512,384]{1,0:T(8,128)(2,1)}, bf16[512,384]{1,0:T(8,128)(2,1)S(1)}, u32[]{:S(2)}, u32[]{:S(2)}) collective-permute-start(bf16[512,384]{1,0:T(8,128)(2,1)} %get-tuple-element.140), channel_id=1, source_target_pairs={{1,0},{9,1},{3,2},{11,3},{5,4},{13,5},{7,6},{15,7},{16,8},{24,9},{... | collective-permute-start | bytes 1179656 | tf_op jit(solution)/shard_map/ppermute | solution.py:277
  136.4 36.7 %collective-permute-start.12 = (bf16[512,384]{1,0:T(8,128)(2,1)}, bf16[512,384]{1,0:T(8,128)(2,1)S(1)}, u32[]{:S(2)}, u32[]{:S(2)}) collective-permute-start(bf16[512,384]{1,0:T(8,128)(2,1)} %get-tuple-element.139), channel_id=1, source_target_pairs={{16,0},{24,1},{18,2},{26,3},{20,4},{28,5},{22,6},{30,7},{17,8},{25... | collective-permute-start | bytes 1179656 | tf_op jit(solution)/shard_map/ppermute | solution.py:277
  137.9 35.4 %collective-permute-start.13 = (bf16[512,384]{1,0:T(8,128)(2,1)}, bf16[512,384]{1,0:T(8,128)(2,1)S(1)}, u32[]{:S(2)}, u32[]{:S(2)}) collective-permute-start(bf16[512,384]{1,0:T(8,128)(2,1)} %get-tuple-element.138), channel_id=1, source_target_pairs={{17,0},{25,1},{19,2},{27,3},{21,4},{29,5},{23,6},{31,7},{0,8},{8,9... | collective-permute-start | bytes 1179656 | tf_op jit(solution)/shard_map/ppermute | solution.py:277
  266.1 19.4 %collective-permute-start.15 = (bf16[512,384]{1,0:T(8,128)(2,1)S(1)}, bf16[512,384]{1,0:T(8,128)(2,1)}, u32[]{:S(2)}, u32[]{:S(2)}) collective-permute-start(bf16[512,384]{1,0:T(8,128)(2,1)S(1)} %get-tuple-element.126), channel_id=1, source_target_pairs={{0,1},{1,9},{2,3},{3,11},{4,5},{5,13},{6,7},{7,15},{8,16},{9,24},{... | collective-permute-start | bytes 1179656 | tf_op jit(solution)/shard_map/ppermute | solution.py:274
  266.1 27.9 %collective-permute-start.16 = (bf16[512,384]{1,0:T(8,128)(2,1)S(1)}, bf16[512,384]{1,0:T(8,128)(2,1)}, u32[]{:S(2)}, u32[]{:S(2)}) collective-permute-start(bf16[512,384]{1,0:T(8,128)(2,1)S(1)} %get-tuple-element.125), channel_id=1, source_target_pairs={{0,16},{1,24},{2,18},{3,26},{4,20},{5,28},{6,22},{7,30},{8,17},{9,... | collective-permute-start | bytes 1179656 | tf_op jit(solution)/shard_map/ppermute | solution.py:274
  267.7 26.4 %collective-permute-start.17 = (bf16[512,384]{1,0:T(8,128)(2,1)S(1)}, bf16[512,384]{1,0:T(8,128)(2,1)}, u32[]{:S(2)}, u32[]{:S(2)}) collective-permute-start(bf16[512,384]{1,0:T(8,128)(2,1)S(1)} %get-tuple-element.124), channel_id=1, source_target_pairs={{0,17},{1,25},{2,19},{3,27},{4,21},{5,29},{6,23},{7,31},{8,0},{9,8... | collective-permute-start | bytes 1179656 | tf_op jit(solution)/shard_map/ppermute | solution.py:274
  388.6 128.1 %reduce-scatter.5.cloned.1.call-start = ((), (), s32[]{:S(2)}) async-start(), calls=%async_computation.6 | async-start | bytes 12165120 | tf_op jit(solution)/shard_map/reduce_scatter | solution.py:466
  389.2 236.8 %all-reduce.7.cloned.1.call-start = ((), (), s32[]{:S(2)}) async-start(), calls=%async_computation.8 | async-start | bytes 3661824 | tf_op jit(solution)/shard_map/psum | solution.py:502
  395.5 121.2 %collective-permute-start.18 = (bf16[1024,768]{1,0:T(8,128)(2,1)}, bf16[1024,768]{1,0:T(8,128)(2,1)}, u32[]{:S(2)}, u32[]{:S(2)}) collective-permute-start(bf16[1024,768]{1,0:T(8,128)(2,1)} %convolution_convert_fusion.3), channel_id=1, source_target_pairs={{0,1},{1,0},{2,3},{3,2},{4,5},{5,4},{6,7},{7,6},{8,9},{9,8},{10,11... | collective-permute-start | bytes 4718600 | tf_op jit(solution)/shard_map/ppermute | solution.py:280
  526.9 19.0 %collective-permute-start.20 = (bf16[1,256,768]{2,1,0:T(8,128)(2,1)}, bf16[1,256,768]{2,1,0:T(8,128)(2,1)}, u32[]{:S(2)}, u32[]{:S(2)}) collective-permute-start(bf16[1,256,768]{2,1,0:T(8,128)(2,1)} %get-tuple-element.121), channel_id=1, source_target_pairs={{1,0},{9,1},{3,2},{11,3},{5,4},{13,5},{7,6},{15,7},{16,8},{24,9},{... | collective-permute-start | bytes 1179656 | tf_op jit(solution)/shard_map/ppermute | solution.py:277
  527.7 62.7 %collective-permute-start.21 = (bf16[1,256,768]{2,1,0:T(8,128)(2,1)}, bf16[1,256,768]{2,1,0:T(8,128)(2,1)}, u32[]{:S(2)}, u32[]{:S(2)}) collective-permute-start(bf16[1,256,768]{2,1,0:T(8,128)(2,1)} %get-tuple-element.120), channel_id=1, source_target_pairs={{16,0},{24,1},{18,2},{26,3},{20,4},{28,5},{22,6},{30,7},{17,8},{25... | collective-permute-start | bytes 1179656 | tf_op jit(solution)/shard_map/ppermute | solution.py:277
  529.3 62.1 %collective-permute-start.22 = (bf16[1,256,768]{2,1,0:T(8,128)(2,1)}, bf16[1,256,768]{2,1,0:T(8,128)(2,1)S(1)}, u32[]{:S(2)}, u32[]{:S(2)}) collective-permute-start(bf16[1,256,768]{2,1,0:T(8,128)(2,1)} %get-tuple-element.119), channel_id=1, source_target_pairs={{17,0},{25,1},{19,2},{27,3},{21,4},{29,5},{23,6},{31,7},{0,8},{8,9... | collective-permute-start | bytes 1179656 | tf_op jit(solution)/shard_map/ppermute | solution.py:277
  (36 other events, 282.8 us)
Sparse Core Ops, SparseCore 0:
  20.2 37.4 all-gather.4
  59.6 23.9 all-gather.6
  85.5 38.7 all-gather.8
  126.0 38.8 all-gather.10
  388.7 40.9 reduce-scatter.6
  433.2 83.5 reduce-scatter.4
  519.2 106.7 all-reduce.6
